TPU v7x, 32 devices: a whole 2x2x4 slice. The times are simulated.
32 devices in a mesh: blk: 8 (over z, x), dp: 4 (over y, core).
Axes of the slice: x: 2, y: 2, z: 4, core: 2. Of those that a mesh axis runs over, the one named last changes fastest.
Arguments:
- tokens: bfloat16 [4096, 3072], P(('blk', 'dp')), may hold values from -6 to 6
- expert_ids: int32 [4096, 2], P(('blk', 'dp')), may hold values from 0 to 7, as said below
- gate_num: int32 [4096], P(('blk', 'dp')), may hold values from 1 to 255
- gate_weight: bfloat16 [3072, 8192], P('dp', 'blk'), may hold values from -0.109375 to 0.109375
- up_weight: bfloat16 [3072, 8192], P('dp', 'blk'), may hold values from -0.109375 to 0.109375
- down_weight: bfloat16 [8192, 3072], P(('blk', 'dp')), may hold values from -0.0625 to 0.0625
Outputs:
- moe_out: bfloat16 [4096, 3072], P(('blk', 'dp'))
Inputs may be any that keep to these rules, and one draw needn't show every extreme that they name: `expert_ids`: each row names two different experts. Among the 128 rows of one device (aligned blocks), between 1 and 64 name expert 0, and in every draw the rows of some device include exactly 64 such rows.
All inputs are finite; a program needn't handle non-finite values.
Results may differ from a plain program's by a relative error of at most 0.018.
Values may be sent and summed in bfloat16 or wider, within the bound.
A program may use at most 192 MiB of HBM per device.

v0:
```python
import jax
import jax.numpy as jnp
from jax import lax
from jax.sharding import PartitionSpec as P

GATE_SCALE = 256.0


def route_table(expert_ids, slot_count):
    hits = jnp.sum((expert_ids == 0).astype(jnp.int32), axis=1)
    position = jnp.cumsum(hits) - 1
    marks = (hits[:, None] > 0) & (
        position[:, None] == jnp.arange(slot_count, dtype=jnp.int32)[None, :]
    )
    return marks.astype(jnp.float32)


def gate_values(expert_ids, gate_num):
    first = gate_num.astype(jnp.float32) / GATE_SCALE
    return jnp.where(expert_ids[:, 0] == 0, first, 0.0) + jnp.where(
        expert_ids[:, 1] == 0, 1.0 - first, 0.0
    )


def on_device(tokens, expert_ids, gate_num, gate_weight, up_weight, down_weight):
    slot_count = tokens.shape[0] // 2
    marks = route_table(expert_ids, slot_count)
    packed = lax.dot_general(
        marks.astype(jnp.bfloat16),
        tokens,
        (((0,), (0,)), ((), ())),
        preferred_element_type=jnp.float32,
    ).astype(jnp.bfloat16)
    down_local = lax.all_gather(down_weight, "dp", axis=0, tiled=True)
    gathered = lax.all_gather(packed, "blk", axis=0, tiled=True)

    def add_rows(piece):
        return jnp.dot(gathered, piece, preferred_element_type=jnp.float32)

    gate = add_rows(lax.all_gather(gate_weight, "dp", axis=0, tiled=True))
    up = add_rows(lax.all_gather(up_weight, "dp", axis=0, tiled=True))
    hidden = (jax.nn.silu(gate) * up).astype(jnp.bfloat16)
    term = jnp.dot(hidden, down_local, preferred_element_type=jnp.float32).astype(jnp.bfloat16)
    term = lax.optimization_barrier(term)
    own_rows = lax.psum_scatter(
        term.astype(jnp.float32).astype(jnp.bfloat16), "blk", scatter_dimension=0, tiled=True
    ).astype(jnp.float32)
    expanded = jnp.dot(marks, own_rows, precision=lax.Precision.HIGHEST)
    weights = gate_values(expert_ids, gate_num)
    return (weights[:, None] * expanded).astype(jnp.bfloat16)


def solution(mesh):
    return jax.shard_map(
        on_device,
        mesh=mesh,
        in_specs=(
            P(("blk", "dp"), None),
            P(("blk", "dp"), None),
            P(("blk", "dp")),
            P("dp", "blk"),
            P("dp", "blk"),
            P(("blk", "dp"), None),
        ),
        out_specs=P(("blk", "dp"), None),
        check_vma=False,
    )
```

profile of v0, /device:TPU:0, one launch (start us, length us, event | category | flops | bytes accessed | tf_op | source)
XLA Modules:
  0.0 311.9 jit_solution(8863363476095033535)
XLA Ops:
  6.5 0.0 copy-start
  6.5 0.0 all-gather.5.cloned.1.call-start
  6.5 0.8 fusion.7
  7.3 0.1 copy.8
  7.4 0.2 reduce-window.8
  7.6 0.1 add_reduce_fusion
  7.7 0.0 copy-done
  7.7 1.1 convolution_convert_fusion.1
  8.9 0.0 all-gather.5.cloned.1.call-update
  8.9 0.0 all-gather.7.cloned.1.call-start
  8.9 0.7 all-gather.7.cloned.1.call-update
  9.6 0.0 all-gather.11.cloned.1.call-start
  9.7 0.7 all-gather.11.cloned.1.call-update
  10.4 0.0 all-gather.9.cloned.1.call-start
  10.4 0.5 all-gather.9.cloned.1.call-update
  10.9 0.0 reduce-scatter.2.cloned.1.call-start
  11.0 61.3 %all-gather.5.cloned.1.call-done = bf16[512,3072]{1,0:T(8,128)(2,1)} async-done(((bf16[64,3072]{1,0:T(8,128)(2,1)}), bf16[512,3072]{1,0:T(8,128)(2,1)}) %all-gather.5.cloned.1.call-update) | async-done | bytes 3145744 | tf_op jit(solution)/shard_map/all_gather | solution.py:35
  72.3 46.6 %all-gather.7.cloned.1.call-done = bf16[3072,1024]{1,0:T(8,128)(2,1)} async-done(((bf16[768,1024]{1,0:T(8,128)(2,1)}), bf16[3072,1024]{1,0:T(8,128)(2,1)}) %all-gather.7.cloned.1.call-update) | async-done | bytes 6291472 | tf_op jit(solution)/shard_map/all_gather | solution.py:40
  118.9 6.4 %fusion.10 = f32[512,1024]{1,0:T(8,128)S(1)} fusion(bf16[512,3072]{1,0:T(8,128)(2,1)} %all-gather.5.cloned.1.call-done, bf16[3072,1024]{1,0:T(8,128)(2,1)} %all-gather.7.cloned.1.call-done), kind=kOutput, calls=%fused_computation.20 | convolution fusion | flops 3221225472 | bytes 11534336 | tf_op jit(solution)/shard_map/dot_general | solution.py:38
  125.4 41.5 %all-gather.11.cloned.1.call-done = bf16[1024,3072]{1,0:T(8,128)(2,1)} async-done(((bf16[256,3072]{1,0:T(8,128)(2,1)}), bf16[1024,3072]{1,0:T(8,128)(2,1)}) %all-gather.11.cloned.1.call-update) | async-done | bytes 6291472 | tf_op jit(solution)/shard_map/all_gather | solution.py:34
  166.9 47.8 %all-gather.9.cloned.1.call-done = bf16[3072,1024]{1,0:T(8,128)(2,1)} async-done(((bf16[768,1024]{1,0:T(8,128)(2,1)}), bf16[3072,1024]{1,0:T(8,128)(2,1)}) %all-gather.9.cloned.1.call-update) | async-done | bytes 6291472 | tf_op jit(solution)/shard_map/all_gather | solution.py:41
  214.7 14.0 %convolution_convert_fusion = bf16[512,3072]{1,0:T(8,128)(2,1)} fusion(bf16[1024,3072]{1,0:T(8,128)(2,1)} %all-gather.11.cloned.1.call-done, f32[512,1024]{1,0:T(8,128)S(1)} %fusion.10, bf16[512,3072]{1,0:T(8,128)(2,1)} %all-gather.5.cloned.1.call-done, bf16[3072,1024]{1,0:T(8,128)(2,1)} %all-gather.9.cloned.1.call-done), kind=kOutput, calls=%fused_computation | convolution fusion | flops 6447169536 | bytes 20971520 | tf_op jit(solution)/shard_map/dot_general | solution.py:43
  228.6 0.0 copy-start.1
  228.6 0.0 copy-start.2
  228.6 0.0 reduce-scatter.2.cloned.1.call-update
  228.7 0.7 copy-done.1
  229.3 0.0 copy-done.2
  229.3 73.7 %reduce-scatter.2.cloned.1.call-done = bf16[64,3072]{1,0:T(8,128)(2,1)} async-done(((bf16[512,3072]{1,0:T(8,128)(2,1)}), bf16[64,3072]{1,0:T(8,128)(2,1)}) %reduce-scatter.2.cloned.1.call-update) | async-done | bytes 393232 | tf_op jit(solution)/shard_map/reduce_scatter | solution.py:45
  303.1 2.3 fusion
  (2 shorter events, 0.0 us)
Async XLA Ops:
  6.5 1.2 copy-start
  6.5 65.7 %all-gather.5.cloned.1.call-start = ((), (), s32[]{:S(2)}) async-start(), calls=%async_computation.1 | async-start | bytes 3538944 | tf_op jit(solution)/shard_map/all_gather | solution.py:35
  8.9 110.0 %all-gather.7.cloned.1.call-start = ((), (), s32[]{:S(2)}) async-start(), calls=%async_computation.2 | async-start | bytes 7864320 | tf_op jit(solution)/shard_map/all_gather | solution.py:40
  9.6 157.2 %all-gather.11.cloned.1.call-start = ((), (), s32[]{:S(2)}) async-start(), calls=%async_computation.4 | async-start | bytes 7864320 | tf_op jit(solution)/shard_map/all_gather | solution.py:34
  10.4 204.3 %all-gather.9.cloned.1.call-start = ((), (), s32[]{:S(2)}) async-start(), calls=%async_computation.3 | async-start | bytes 7864320 | tf_op jit(solution)/shard_map/all_gather | solution.py:41
  10.9 292.1 %reduce-scatter.2.cloned.1.call-start = ((), (), s32[]{:S(2)}) async-start(), calls=%async_computation.5 | async-start | bytes 3538944 | tf_op jit(solution)/shard_map/reduce_scatter | solution.py:45
  228.6 0.7 copy-start.1
  228.6 0.7 copy-start.2
Sparse Core Ops, SparseCore 0:
  9.5 62.7 all-gather.4
  73.8 45.0 all-gather.6
  120.5 46.3 all-gather.10
  168.3 46.3 all-gather.8
  228.8 74.2 reduce-scatter.1
where the time goes:
time: 312 us
  waiting for transfers between devices  273 us (88%)
  matrix products  23.8 us (8%)
  between operations  13.2 us (4%)
    reduce_scatter x1, waiting for transfers between devices, on_device(): lax.psum_scatter(term.astype(jnp.float32).astype(jnp.bfloat16), 'blk', sc...  73.7 us
    all_gather x1, waiting for transfers between devices, on_device(): gathered = lax.all_gather(packed, 'blk', axis=0, tiled=True)  61.3 us
    all_gather x1, waiting for transfers between devices, on_device(): up = add_rows(lax.all_gather(up_weight, 'dp', axis=0, tiled=True))  47.8 us
    all_gather x1, waiting for transfers between devices, on_device(): gate = add_rows(lax.all_gather(gate_weight, 'dp', axis=0, tiled=True))  46.6 us
    all_gather x1, waiting for transfers between devices, on_device(): down_local = lax.all_gather(down_weight, 'dp', axis=0, tiled=True)  41.5 us
    dot_general x1, matrix products, on_device(): jnp.dot(hidden, down_local, preferred_element_type=jnp.float32)  14 us
    dot_general x1, matrix products, add_rows(): return jnp.dot(gathered, piece, preferred_element_type=jnp.float32)  6.44 us
  transfers between devices with their start and end apart: 5, of which 5 were waited for; matrix products, arithmetic and copies ran while one was open for 2% of the time, Pallas kernels for 0%

commit v1 on v0

--- a/solution.py
+++ b/solution.py
@@ -31,7 +31,12 @@
         (((0,), (0,)), ((), ())),
         preferred_element_type=jnp.float32,
     ).astype(jnp.bfloat16)
-    down_local = lax.all_gather(down_weight, "dp", axis=0, tiled=True)
+    ring = [down_weight]
+    for hop in range(3):
+        ring.append(lax.ppermute(ring[-1], "dp", [(dev, (dev + 1) % 4) for dev in range(4)]))
+    down_local = jnp.roll(
+        jnp.concatenate(ring[::-1], axis=0), (lax.axis_index("dp") + 1) * ring[0].shape[0], axis=0
+    )
     gathered = lax.all_gather(packed, "blk", axis=0, tiled=True)
 
     def add_rows(piece):

time: 312 us -> 265 us (0.85)
  waiting for transfers between devices: 273 us -> 205 us
  local copies, waits for them, and re-layouts: 0.77 us -> 18.1 us
    all_gather x1, waiting for transfers between devices: 61.3 us -> 0.01 us  [on_device(): gathered = lax.all_gather(packed, 'blk', axis=0, tiled=True)]
    ppermute x0 -> x3, waiting for transfers between devices: none -> 60.1 us  [on_device(): lax.ppermute(ring[-1], 'dp', [(dev, (dev + 1) % 4) for dev in range(4)])]
    all_gather x1 -> x0, waiting for transfers between devices: 41.5 us -> none  [on_device(): down_local = lax.all_gather(down_weight, 'dp', axis=0, tiled=True)]
    all_gather x1, waiting for transfers between devices: 46.6 us -> 30.4 us  [on_device(): gate = add_rows(lax.all_gather(gate_weight, 'dp', axis=0, tiled=True))]
    unnamed x6 -> x19, local copies, waits for them, and re-layouts: 0.66 us -> 16.7 us
    all_gather x1, waiting for transfers between devices: 47.8 us -> 39.4 us  [on_device(): up = add_rows(lax.all_gather(up_weight, 'dp', axis=0, tiled=True))]
  transfers between devices with their start and end apart: 5 -> 7, of which waited for: 5 -> 6; matrix products, arithmetic and copies ran while one was open for 2% -> 9% of each run, Pallas kernels for 0% -> 0%
where the time goes in v1:
time: 265 us
  waiting for transfers between devices  205 us (77%)
  matrix products  26.5 us (10%)
  local copies, waits for them, and re-layouts  18.1 us (7%)
  between operations  13.2 us (5%)
    reduce_scatter x1, waiting for transfers between devices, on_device(): lax.psum_scatter(term.astype(jnp.float32).astype(jnp.bfloat16), 'blk', sc...  73.9 us
    ppermute x3, waiting for transfers between devices, on_device(): lax.ppermute(ring[-1], 'dp', [(dev, (dev + 1) % 4) for dev in range(4)])  60.1 us
    all_gather x1, waiting for transfers between devices, on_device(): up = add_rows(lax.all_gather(up_weight, 'dp', axis=0, tiled=True))  39.4 us
    all_gather x1, waiting for transfers between devices, on_device(): gate = add_rows(lax.all_gather(gate_weight, 'dp', axis=0, tiled=True))  30.4 us
    unnamed x19, local copies, waits for them, and re-layouts  16.7 us
    dot_general x1, matrix products, on_device(): jnp.dot(hidden, down_local, preferred_element_type=jnp.float32)  14.5 us
    dot_general x1, matrix products, add_rows(): return jnp.dot(gathered, piece, preferred_element_type=jnp.float32)  8.58 us
  transfers between devices with their start and end apart: 7, of which 6 were waited for; matrix products, arithmetic and copies ran while one was open for 9% of the time, Pallas kernels for 0%

profile of v1, /device:TPU:0, one launch (start us, length us, event | category | flops | bytes accessed | tf_op | source)
XLA Modules:
  0.0 264.7 jit_solution(4907145526455168116)
XLA Ops:
  6.5 0.0 copy-start
  6.5 0.0 copy-start.1
  6.5 0.0 all-gather.4.cloned.1.call-start
  6.5 0.8 fusion.12
  7.4 0.1 copy.8
  7.5 0.2 reduce-window.8
  7.7 0.1 add_reduce_fusion
  7.8 0.0 copy-done
  7.8 1.1 convolution_convert_fusion
  8.9 0.0 all-gather.4.cloned.1.call-update
  9.0 0.0 all-gather.6.cloned.1.call-start
  9.0 0.7 all-gather.6.cloned.1.call-update
  9.7 0.0 all-gather.8.cloned.1.call-start
  9.8 0.7 all-gather.8.cloned.1.call-update
  10.4 0.0 reduce-scatter.2.cloned.1.call-start
  10.5 0.0 copy-done.1
  10.5 0.5 collective-permute-start
  11.0 20.0 %collective-permute-done = bf16[256,3072]{1,0:T(8,128)(2,1)S(1)} collective-permute-done((bf16[256,3072]{1,0:T(8,128)(2,1)S(1)}, bf16[256,3072]{1,0:T(8,128)(2,1)S(1)}, u32[]{:S(2)}, u32[]{:S(2)}) %collective-permute-start) | collective-permute-done | bytes 1572896 | tf_op jit(solution)/shard_map/ppermute | solution.py:36
  31.1 0.0 copy-start.2
  31.1 1.2 copy-done.2
  32.3 0.0 collective-permute-start.1
  32.3 19.9 %collective-permute-done.1 = bf16[256,3072]{1,0:T(8,128)(2,1)} collective-permute-done((bf16[256,3072]{1,0:T(8,128)(2,1)S(1)}, bf16[256,3072]{1,0:T(8,128)(2,1)}, u32[]{:S(2)}, u32[]{:S(2)}) %collective-permute-start.1) | collective-permute-done | bytes 1572896 | tf_op jit(solution)/shard_map/ppermute | solution.py:36
  52.2 0.0 collective-permute-start.2
  52.2 0.0 copy-start.3
  52.2 20.2 %collective-permute-done.2 = bf16[256,3072]{1,0:T(8,128)(2,1)} collective-permute-done((bf16[256,3072]{1,0:T(8,128)(2,1)}, bf16[256,3072]{1,0:T(8,128)(2,1)}, u32[]{:S(2)}, u32[]{:S(2)}) %collective-permute-start.2) | collective-permute-done | bytes 1572896 | tf_op jit(solution)/shard_map/ppermute | solution.py:36
  72.4 2.7 %constant_dynamic-update-slice_fusion.7 = bf16[2048,3072]{1,0:T(8,128)(2,1)} fusion(bf16[256,3072]{1,0:T(8,128)(2,1)} %collective-permute-done.2), kind=kLoop, calls=%fused_computation.22 | loop fusion | bytes 3145728
  75.0 2.7 %constant_dynamic-update-slice_fusion.6 = bf16[2048,3072]{1,0:T(8,128)(2,1)} fusion(bf16[2048,3072]{1,0:T(8,128)(2,1)} %constant_dynamic-update-slice_fusion.7, bf16[256,3072]{1,0:T(8,128)(2,1)} %collective-permute-done.1), kind=kLoop, calls=%fused_computation.21 | loop fusion | bytes 3145728
  77.7 0.0 copy-done.3
  77.7 1.3 constant_dynamic-update-slice_fusion.5
  78.9 1.3 constant_dynamic-update-slice_fusion.4
  80.2 2.9 %constant_dynamic-update-slice_fusion.3 = bf16[2048,3072]{1,0:T(8,128)(2,1)} fusion(bf16[2048,3072]{1,0:T(8,128)(2,1)} %constant_dynamic-update-slice_fusion.4, bf16[256,3072]{1,0:T(8,128)(2,1)} %collective-permute-done.2), kind=kLoop, calls=%fused_computation.18 | loop fusion | bytes 3145728
  83.1 2.9 %constant_dynamic-update-slice_fusion.2 = bf16[2048,3072]{1,0:T(8,128)(2,1)} fusion(bf16[2048,3072]{1,0:T(8,128)(2,1)} %constant_dynamic-update-slice_fusion.3, bf16[256,3072]{1,0:T(8,128)(2,1)} %collective-permute-done.1), kind=kLoop, calls=%fused_computation.17 | loop fusion | bytes 3145728
  86.0 1.3 constant_dynamic-update-slice_fusion.1
  87.2 1.3 constant_dynamic-update-slice_fusion
  88.5 0.0 all-gather.4.cloned.1.call-done
  88.5 30.4 %all-gather.6.cloned.1.call-done = bf16[3072,1024]{1,0:T(8,128)(2,1)} async-done(((bf16[768,1024]{1,0:T(8,128)(2,1)}), bf16[3072,1024]{1,0:T(8,128)(2,1)}) %all-gather.6.cloned.1.call-update) | async-done | bytes 6291472 | tf_op jit(solution)/shard_map/all_gather | solution.py:45
  118.9 8.6 %fusion.16 = f32[512,1024]{1,0:T(8,128)} fusion(bf16[512,3072]{1,0:T(8,128)(2,1)} %all-gather.4.cloned.1.call-done, bf16[3072,1024]{1,0:T(8,128)(2,1)} %all-gather.6.cloned.1.call-done), kind=kOutput, calls=%fused_computation.31 | convolution fusion | flops 3221225472 | bytes 11534336 | tf_op jit(solution)/shard_map/dot_general | solution.py:43
  127.5 39.4 %all-gather.8.cloned.1.call-done = bf16[3072,1024]{1,0:T(8,128)(2,1)} async-done(((bf16[768,1024]{1,0:T(8,128)(2,1)}), bf16[3072,1024]{1,0:T(8,128)(2,1)}) %all-gather.8.cloned.1.call-update) | async-done | bytes 6291472 | tf_op jit(solution)/shard_map/all_gather | solution.py:46
  166.9 14.5 %fusion.2 = bf16[512,3072]{1,0:T(8,128)(2,1)} fusion(bf16[2048,3072]{1,0:T(8,128)(2,1)} %constant_dynamic-update-slice_fusion, s32[]{:T(128)S(6)} %select_n.23, f32[512,1024]{1,0:T(8,128)} %fusion.16, bf16[512,3072]{1,0:T(8,128)(2,1)} %all-gather.4.cloned.1.call-done, bf16[3072,1024]{1,0:T(8,128)(2,1)} %all-gather.8.cloned.1.call-done), kind=kOutput, calls=%fused_computation.2 | convolution fusion | flops 6447169536 | bytes 20971524 | tf_op jit(solution)/shard_map/dot_general | solution.py:48
  181.4 0.0 copy-start.4
  181.4 0.0 copy-start.5
  181.4 0.0 reduce-scatter.2.cloned.1.call-update
  181.4 0.7 copy-done.4
  182.0 0.0 copy-done.5
  182.0 73.9 %reduce-scatter.2.cloned.1.call-done = bf16[64,3072]{1,0:T(8,128)(2,1)} async-done(((bf16[512,3072]{1,0:T(8,128)(2,1)}), bf16[64,3072]{1,0:T(8,128)(2,1)}) %reduce-scatter.2.cloned.1.call-update) | async-done | bytes 393232 | tf_op jit(solution)/shard_map/reduce_scatter | solution.py:50
  255.9 2.3 fusion.5
  (2 shorter events, 0.0 us)
Async XLA Ops:
  6.5 1.3 copy-start
  6.5 4.0 %copy-start.1 = (bf16[256,3072]{1,0:T(8,128)(2,1)S(1)}, bf16[256,3072]{1,0:T(8,128)(2,1)}, u32[]{:S(2)}) copy-start(bf16[256,3072]{1,0:T(8,128)(2,1)} %param.11) | copy-start | bytes 4718596
  6.5 81.9 %all-gather.4.cloned.1.call-start = ((), (), s32[]{:S(2)}) async-start(), calls=%async_computation.1 | async-start | bytes 3538944 | tf_op jit(solution)/shard_map/all_gather | solution.py:40
  9.0 109.9 %all-gather.6.cloned.1.call-start = ((), (), s32[]{:S(2)}) async-start(), calls=%async_computation.2 | async-start | bytes 7864320 | tf_op jit(solution)/shard_map/all_gather | solution.py:45
  9.7 157.2 %all-gather.8.cloned.1.call-start = ((), (), s32[]{:S(2)}) async-start(), calls=%async_computation.3 | async-start | bytes 7864320 | tf_op jit(solution)/shard_map/all_gather | solution.py:46
  10.4 245.5 %reduce-scatter.2.cloned.1.call-start = ((), (), s32[]{:S(2)}) async-start(), calls=%async_computation.4 | async-start | bytes 3538944 | tf_op jit(solution)/shard_map/reduce_scatter | solution.py:50
  10.5 20.6 %collective-permute-start = (bf16[256,3072]{1,0:T(8,128)(2,1)S(1)}, bf16[256,3072]{1,0:T(8,128)(2,1)S(1)}, u32[]{:S(2)}, u32[]{:S(2)}) collective-permute-start(bf16[256,3072]{1,0:T(8,128)(2,1)S(1)} %copy-done.1), channel_id=1, source_target_pairs={{0,1},{1,2},{2,3},{3,0},{4,5},{5,6},{6,7},{7,4},{8,9},{9,10},{10,1... | collective-permute-start | bytes 4718600 | tf_op jit(solution)/shard_map/ppermute | solution.py:36
  31.1 1.2 copy-start.2
  32.3 19.9 %collective-permute-start.1 = (bf16[256,3072]{1,0:T(8,128)(2,1)S(1)}, bf16[256,3072]{1,0:T(8,128)(2,1)}, u32[]{:S(2)}, u32[]{:S(2)}) collective-permute-start(bf16[256,3072]{1,0:T(8,128)(2,1)S(1)} %collective-permute-done), channel_id=1, source_target_pairs={{0,1},{1,2},{2,3},{3,0},{4,5},{5,6},{6,7},{7,4},{8,9},{9,10},{10,1... | collective-permute-start | bytes 4718600 | tf_op jit(solution)/shard_map/ppermute | solution.py:36
  52.2 20.2 %collective-permute-start.2 = (bf16[256,3072]{1,0:T(8,128)(2,1)}, bf16[256,3072]{1,0:T(8,128)(2,1)}, u32[]{:S(2)}, u32[]{:S(2)}) collective-permute-start(bf16[256,3072]{1,0:T(8,128)(2,1)} %collective-permute-done.1), channel_id=1, source_target_pairs={{0,1},{1,2},{2,3},{3,0},{4,5},{5,6},{6,7},{7,4},{8,9},{9,10},{10,1... | collective-permute-start | bytes 4718600 | tf_op jit(solution)/shard_map/ppermute | solution.py:36
  52.2 25.5 %copy-start.3 = (bf16[256,3072]{1,0:T(8,128)(2,1)S(1)}, bf16[256,3072]{1,0:T(8,128)(2,1)}, u32[]{:S(2)}) copy-start(bf16[256,3072]{1,0:T(8,128)(2,1)} %copy-done.2) | copy-start | bytes 4718596
  181.4 0.7 copy-start.4
  181.4 0.7 copy-start.5
Sparse Core Ops, SparseCore 0:
  9.5 62.7 all-gather.3
  73.8 45.0 all-gather.5
  120.5 46.3 all-gather.7
  181.5 74.3 reduce-scatter.1
